TPU v7x, 32 devices: a whole 2x2x4 slice. The times are simulated.
32 devices in a mesh: col: 4 (over y, x), row: 8 (over z, core).
Axes of the slice: x: 2, y: 2, z: 4, core: 2. Of those that a mesh axis runs over, the one named last changes fastest.
Arguments:
- data: bfloat16 [16384, 8192], P('row', 'col'), may hold values from -6 to 6
- column_scale: float32 [8192], P('col'), may hold values from 0.25 to 4
- keep_mask: int32 [16384, 8192], P('row', 'col'), may hold values 0 or 1
Outputs:
- band: float32 [8192, 3, 2048], P('col', None, 'row')
All inputs are finite; a program needn't handle non-finite values. No bound on the sum of `keep_mask` on one device may be relied on, other than what follows from the above.
Results may differ from a plain program's by a relative error of at most 0.0012.
Values may be sent and summed in bfloat16 or wider, within the bound.
A program may use at most 128 MiB of HBM per device.

v0:
```python
import functools

import jax
import jax.numpy as jnp
from jax import lax
from jax.experimental import pallas as pl
from jax.experimental.pallas import tpu as pltpu
from jax.experimental.layout import Layout, with_layout_constraint
from jax.sharding import PartitionSpec as P


CHUNKS = 2
TOP = 16384.0


def passed_along(block, axis, distance):
    size = lax.axis_size(axis)
    return lax.ppermute(block, axis, [((i - distance) % size, i) for i in range(size)])


def swapped(block, axis):
    return lax.ppermute(block, axis, [(i, i ^ 1) for i in range(lax.axis_size(axis))])


def product(left, right):
    return lax.dot_general(
        left, right, (((0,), (0,)), ((), ())), preferred_element_type=jnp.float32
    )


def chunk_of(block, owners, q):
    width = block.shape[-1] // (owners * CHUNKS)
    starts = [(owner * CHUNKS + q) * width for owner in range(owners)]
    return jnp.concatenate([block[..., s:s + width] for s in starts], axis=-1)


def summed_over_rows(partial, pairs):
    me = lax.axis_index("row")
    pair, half = me // 2, me % 2
    parts = partial.reshape((pairs, 2, -1) + partial.shape[1:])
    mine = lax.dynamic_index_in_dim(parts, half, 1, keepdims=False)
    theirs = lax.dynamic_index_in_dim(parts, 1 - half, 1, keepdims=False)
    from_partner = swapped(theirs, "row")

    def both(at):
        one, two = (
            lax.dynamic_index_in_dim(a, at % pairs, 0, keepdims=False).astype(jnp.float32)
            for a in (mine, from_partner)
        )
        return one + two

    total = both(pair)
    plain = Layout(major_to_minor=(0, 1))
    blocks = [
        with_layout_constraint(both(pair + step).astype(jnp.float16), plain)
        for step in range(1, pairs)
    ]
    for step, block in enumerate(blocks, 1):
        arrived = with_layout_constraint(passed_along(block, "row", 2 * step), plain)
        total = total + arrived.astype(jnp.float32)
    return total, blocks


def on_device(data, column_scale, keep_mask):
    rows = lax.axis_size("row")
    n_col = lax.axis_size("col")
    offsets = n_col // 2 + 1
    values = data.astype(jnp.float32) * column_scale[None, :]
    colsq = lax.psum(jnp.sum(values * values, axis=0), "row")
    total_rows = data.shape[0] * rows
    divisor = jnp.minimum(jnp.sqrt(colsq + 1.0), jnp.sqrt(jnp.float32(total_rows)))
    norm = jnp.sqrt(jnp.maximum(colsq, 1e-30)) / divisor
    norms = [norm] + [passed_along(norm, "col", -offset) for offset in range(1, offsets)]
    divisor, norms = lax.optimization_barrier((divisor, norms))
    scaled = (keep_mask.astype(jnp.float32) * values / divisor[None, :]).astype(jnp.bfloat16)
    even = lax.axis_index("col") % 2 == 0

    own = [chunk_of(scaled, rows, q) for q in range(CHUNKS)]
    panels = {(0, q): own[q] for q in range(CHUNKS)}
    for q in range(CHUNKS):
        for offset in range(2, offsets, 2):
            panels[offset, q] = passed_along(own[q], "col", -offset)
    gain = TOP / norm
    kept = {}

    def stage(name, panel, length):
        partial = product(panel, scaled) * gain[None, :] * (1.0 / length)[:, None]
        partial = partial.astype(jnp.float16)
        total, blocks = summed_over_rows(partial, rows // 2)
        back = length.reshape(rows, -1)[lax.axis_index("row")]
        kept[name] = total * (norm * (1.0 / TOP))[None, :] * back[:, None]
        return blocks

    blocks = stage("0", scaled, norm)
    for offset in list(range(2, offsets, 2)) + list(range(1, offsets, 2)):
        for q in range(CHUNKS):
            if offset % 2:
                if n_col % 2 == 0 and (offset + 1, q) in panels:
                    after, before = panels[offset + 1, q], panels[offset - 1, q]
                    panels[offset, q] = swapped(jnp.where(even, after, before), "col")
                else:
                    panels[offset, q] = passed_along(own[q], "col", -offset)
            panels[offset, q], blocks = lax.optimization_barrier((panels[offset, q], blocks))
            length = chunk_of(norms[offset], rows, q)
            blocks = stage(f"{offset}_{q}", panels[offset, q], length)
    result = [kept["0"]]
    for offset in range(1, offsets):
        result.append(jnp.concatenate([kept[f"{offset}_{q}"] for q in range(CHUNKS)], axis=0))
    return jnp.stack([total.T for total in result], axis=1)


LANES = 128
SENT_TOP = 1024.0
MESH_ID = pl.DeviceIdType.MESH


def sent(x):
    x = x * jnp.abs(x)
    return (x * jnp.abs(x)).astype(jnp.bfloat16)


def received(y):
    y = y.astype(jnp.float32)
    size = lax.rsqrt(lax.rsqrt(jnp.maximum(jnp.abs(y), 1e-37)))
    return jnp.where(y < 0.0, -size, size)


def square_kernel(
    n_row, data, scale, mask, out,
    buf, own_t, chunk, swap_out, swap_in, hold, near, far, line, masks, sums, plain, vec, back,
    data_sem, mask_sem, sum_send, sum_recv, vec_send, vec_recv, y_send, y_recv, x_send, x_recv,
    swap_send, swap_recv, line_send, near_recv, far_recv, out_sem, near_free,
):
    c, r = lax.axis_index("col"), lax.axis_index("row")
    z, k = r // 2, r % 2
    rows, panel = data.shape
    pairs = n_row // 2
    piece = panel // n_row
    wide = 2 * LANES
    parts = piece // LANES
    chunks = pairs * parts
    block = rows // 4
    half = rows // 2
    last = 3 * chunks + 2
    near_slots, hold_slots, line_slots = 3 * pairs, 7, 4
    forwards = c % 2 == 0
    y_peer, x_peer = (c + 2) % 4, c + 1 - 2 * (c % 2)
    partner = 2 * (z + 1 - 2 * (z % 2)) + k
    inner = jnp.logical_or(z == 1, z == 2)

    def target_of(q):
        at = q % pairs
        return jnp.where(at == 0, 0, jnp.where(at == 1, 3, at - 1))

    def column_of(q, core):
        start = (2 * target_of(q) + core) * piece + (q // pairs) * LANES
        return pl.multiple_of(start, LANES)

    def stage_of(m):
        offset = m % 3
        return offset, m // 3 - jnp.where(offset == 1, 1, 0)

    def valid(m):
        return (m >= 0) & (m < last) & (m != 1) & (m != last - 2)

    def role_of(q):
        goal = target_of(q)
        same = z // 2 == goal // 2
        return jnp.where(z == goal, 3, jnp.where(same, 1, jnp.where(inner, 2, 1)))

    def data_copy(q, side):
        return pltpu.make_async_copy(
            data.at[:, pl.ds(column_of(q, k if side == 0 else 1 - k), LANES)],
            buf.at[0, q, :, pl.ds(side * LANES, LANES)], data_sem.at[q, side])

    def mask_copy(q, side):
        return pltpu.make_async_copy(
            mask.at[:, pl.ds(column_of(q, k if side == 0 else 1 - k), LANES)],
            masks.at[q % 2, :, pl.ds(side * LANES, LANES)], mask_sem.at[q % 2, side])

    def half_of(offset, q, part):
        return buf.at[offset, q, pl.ds(part * half, half), :]

    def y_copy(q, part):
        return pltpu.make_async_remote_copy(
            half_of(0, q, part), half_of(2, q, part), y_send.at[q, part], y_recv.at[q, part],
            device_id=(y_peer, r), device_id_type=MESH_ID)

    def x_copy(q, part, source):
        return pltpu.make_async_remote_copy(
            half_of(source, q, part), half_of(1, q, part), x_send.at[q, part], x_recv.at[q, part],
            device_id=(x_peer, r), device_id_type=MESH_ID)

    def start_own(q):
        for part in range(2):
            y_copy(q, part).start()

            @pl.when(jnp.logical_not(forwards))
            def _():
                x_copy(q, part, 0).start()

    @pl.loop(0, chunks)
    def _(q):
        for side in range(2):
            data_copy(q, side).start()

    for q in range(2):
        for side in range(2):
            mask_copy(q, side).start()

    barrier = pltpu.get_barrier_semaphore()
    for step in range(1, n_row):
        pl.semaphore_signal(barrier, inc=1, device_id=(c, (r + step) % n_row), device_id_type=MESH_ID)
    for step in range(1, 4):
        pl.semaphore_signal(barrier, inc=1, device_id=((c + step) % 4, r), device_id_type=MESH_ID)
    pl.semaphore_wait(barrier, n_row + 2)

    @pl.loop(0, chunks)
    def _(q):
        for side in range(2):
            data_copy(q, side).wait()
            mask_copy(q, side).wait()
        scales = jnp.concatenate(
            [scale[:, pl.ds(column_of(q, k), LANES)], scale[:, pl.ds(column_of(q, 1 - k), LANES)]], axis=1)
        step = 128

        def read(b, total):
            at = pl.ds(pl.multiple_of(b * step, step), step)
            values = buf[0, q, at, :].astype(jnp.float32)
            kept = masks[q % 2, at, :].astype(jnp.float32) * values
            buf[0, q, at, :] = kept.astype(jnp.bfloat16)
            values = values * scales
            return total + jnp.sum((values * values).reshape(step // 8, 8, wide), axis=0)

        total = lax.fori_loop(0, rows // step, read, jnp.zeros((8, wide), jnp.float32))
        total = jnp.sum(total, axis=0, keepdims=True)
        sums[r, :, pl.ds(column_of(q, k), LANES)] = total[:, :LANES]
        sums[r, :, pl.ds(column_of(q, 1 - k), LANES)] = total[:, LANES:]

        @pl.when(q + 2 < chunks)
        def _():
            for side in range(2):
                mask_copy(q + 2, side).start()

        @pl.when(q == 0)
        def _():
            start_own(q)

    def sum_copy(step):
        peer = (r + step) % n_row
        return pltpu.make_async_remote_copy(
            sums.at[r], sums.at[r], sum_send.at[step], sum_recv.at[step],
            device_id=(c, peer), device_id_type=MESH_ID)

    def sum_arrival(step):
        origin = (r + n_row - step) % n_row
        return pltpu.make_async_remote_copy(
            sums.at[origin], sums.at[origin], sum_send.at[step], sum_recv.at[step],
            device_id=(c, origin), device_id_type=MESH_ID)

    for step in range(1, n_row):
        sum_copy(step).start()
    for step in range(1, n_row):
        sum_arrival(step).wait_recv()
    colsq = sums[0]
    for origin in range(1, n_row):
        colsq = colsq + sums[origin]
    divisor = jnp.minimum(jnp.sqrt(colsq + 1.0), jnp.sqrt(jnp.full_like(colsq, rows * n_row)))
    size = jnp.sqrt(jnp.maximum(colsq, 1e-30)) / divisor
    up = jnp.full_like(size, SENT_TOP)
    down = jnp.full_like(size, 1.0 / SENT_TOP)
    for power in (32, 16, 8, 4, 2, 1):
        small = size < 2.0 ** -power
        size = jnp.where(small, size * 2.0 ** power, size)
        up = jnp.where(small, up * 2.0 ** power, up)
        down = jnp.where(small, down * 2.0 ** -power, down)
    plain[0:1, :] = scale[...] / divisor * up
    plain[1:2, :] = down

    @pl.loop(0, chunks)
    def _(q):
        for side in range(2):
            column = column_of(q, k if side == 0 else 1 - k)
            to = pl.ds(pl.multiple_of(q * wide + side * LANES, LANES), LANES)
            vec[0, :, to] = plain[:, pl.ds(column, LANES)]

    def vec_copy(offset):
        return pltpu.make_async_remote_copy(
            vec.at[0], vec.at[offset], vec_send.at[offset], vec_recv.at[offset],
            device_id=((c + 4 - offset) % 4, r), device_id_type=MESH_ID)

    for offset in (2, 1):
        vec_copy(offset).start()

    @pl.loop(1, chunks)
    def _(q):
        start_own(q)

    @pl.loop(0, chunks)
    def _(q):
        for side in range(2):
            column = column_of(q, k if side == 0 else 1 - k)
            lanes = pl.ds(side * LANES, LANES)
            factors = vec[0, :, pl.ds(pl.multiple_of(q * wide + side * LANES, LANES), LANES)]

            @pl.loop(0, rows // block)
            def _(b):
                at = pl.ds(pl.multiple_of(b * block, block), block)
                scaled = (buf[0, q, at, lanes].astype(jnp.float32) * factors[0:1, :]).astype(jnp.bfloat16)
                own_t[pl.ds(column, LANES), at] = scaled.T

            back[pl.ds(column, LANES), :] = jnp.broadcast_to(factors[1:2, :], (LANES, LANES)).T

    for offset in (2, 1):
        vec_copy(offset).wait_recv()

    tall = panel // 4

    def swap_copy(m):
        return pltpu.make_async_remote_copy(
            swap_out.at[m % 2], swap_in.at[m % 4], swap_send.at[m % 2], swap_recv.at[m % 4],
            device_id=(c, 2 * z + 1 - k), device_id_type=MESH_ID)

    def near_copy(m):
        return pltpu.make_async_remote_copy(
            line.at[m % line_slots], near.at[m % near_slots],
            line_send.at[m % line_slots], near_recv.at[m % near_slots],
            device_id=(c, partner), device_id_type=MESH_ID)

    def far_copy(m, offset, q):
        slot = offset * parts + q // pairs
        return pltpu.make_async_remote_copy(
            line.at[m % line_slots], far.at[slot], line_send.at[m % line_slots], far_recv.at[slot],
            device_id=(c, 2 * target_of(q) + k), device_id_type=MESH_ID)

    def out_copy(m, offset, q):
        lanes = pl.ds(pl.multiple_of((q // pairs) * LANES, LANES), LANES)
        return pltpu.make_async_copy(
            hold.at[m % hold_slots], out.at[offset, :, lanes], out_sem.at[m % hold_slots])

    def give_back(m):
        @pl.when(valid(m + near_slots))
        def _():
            pl.semaphore_signal(
                near_free.at[m % near_slots], inc=1, device_id=(c, partner), device_id_type=MESH_ID)

    def in_blocks(body):
        step = 256

        @pl.loop(0, panel // step)
        def _(b):
            body(pl.ds(pl.multiple_of(b * step, step), step))

    @pl.loop(0, last + hold_slots)
    def _(n):
        def settle(m, action):
            offset, q = stage_of(m)

            @pl.when(valid(m))
            def _():
                action(offset, q)

        def close_swap(offset, q):
            swap_copy(n - 2).wait_send()

        def close_out(offset, q):
            @pl.when(role_of(q) == 3)
            def _():
                out_copy(n - hold_slots, offset, q).wait()

        settle(n - 2, close_swap)
        settle(n - hold_slots, close_out)

        def arrive(part):
            q = n // 3
            y_copy(q, part).wait_recv()

            @pl.when(forwards)
            def _():
                x_copy(q, part, 2).start()

        @pl.when((n % 3 == 1) & (n // 3 < chunks))
        def _():
            arrive(0)

        @pl.when((n % 3 == 2) & (n // 3 < chunks))
        def _():
            arrive(1)

        def multiply(offset, q):
            @pl.when(offset == 1)
            def _():
                for part in range(2):
                    x_copy(q, part, 0).wait_recv()

            factors = vec[offset, 0:1, pl.ds(pl.multiple_of(q * wide, wide), wide)]

            @pl.loop(0, rows // block)
            def _(b):
                at = pl.ds(pl.multiple_of(b * block, block), block)
                chunk[at, :] = (buf[offset, q, at, :].astype(jnp.float32) * factors).astype(jnp.bfloat16)

            @pl.loop(0, panel // tall)
            def _(b):
                at = pl.ds(pl.multiple_of(b * tall, tall), tall)
                product = jnp.dot(own_t[at, :], chunk[...], preferred_element_type=jnp.float32)
                hold[n % hold_slots, at, :] = product[:, :LANES]
                swap_out[n % 2, at, :] = product[:, LANES:]

            swap_copy(n).start()

        settle(n, multiply)

        def join(offset, q):
            m = n - 1
            swap_copy(m).wait_recv()
            role = role_of(q)

            @pl.when(role == 1)
            def _():
                def body(at):
                    line[m % line_slots, at, :] = sent(hold[m % hold_slots, at, :] + swap_in[m % 4, at, :])

                in_blocks(body)

                @pl.when(valid(m - near_slots))
                def _():
                    pl.semaphore_wait(near_free.at[m % near_slots], 1)

                near_copy(m).start()

            @pl.when(role != 1)
            def _():
                def body(at):
                    hold[m % hold_slots, at, :] = hold[m % hold_slots, at, :] + swap_in[m % 4, at, :]

                in_blocks(body)

        def close_line(offset, q):
            @pl.when(role_of(q) != 3)
            def _():
                near_copy(n - 1 - line_slots).wait_send()

        settle(n - 1 - line_slots, close_line)
        settle(n - 1, join)

        def relay(offset, q):
            m = n - 3

            @pl.when(role_of(q) == 2)
            def _():
                near_copy(m).wait_recv()

                def body(at):
                    line[m % line_slots, at, :] = sent(
                        hold[m % hold_slots, at, :] + received(near[m % near_slots, at, :]))

                in_blocks(body)
                give_back(m)
                far_copy(m, offset, q).start()

        settle(n - 3, relay)

        def finish(offset, q):
            m = n - 5

            @pl.when(role_of(q) == 3)
            def _():
                near_copy(m).wait_recv()
                far_copy(m, offset, q).wait_recv()
                slot = offset * parts + q // pairs
                factors = vec[offset, 1:2, pl.ds(pl.multiple_of(q * wide, wide), LANES)]

                def body(at):
                    total = hold[m % hold_slots, at, :] + received(near[m % near_slots, at, :])
                    total = total + received(far[slot, at, :])
                    hold[m % hold_slots, at, :] = total * back[at, :] * factors

                in_blocks(body)
                give_back(m)
                out_copy(m, offset, q).start()

        settle(n - 5, finish)

    @pl.loop(0, chunks)
    def _(q):
        for part in range(2):
            y_copy(q, part).wait_send()
            x_copy(q, part, 0).wait_send()

    for step in range(1, n_row):
        sum_copy(step).wait_send()
    for offset in (2, 1):
        vec_copy(offset).wait_send()


def square_program(n_row):
    def on_device(data, column_scale, keep_mask):
        rows, panel = data.shape
        piece = panel // n_row
        pairs, parts = n_row // 2, piece // LANES
        chunks = pairs * parts
        f32, bf16, dma = jnp.float32, jnp.bfloat16, pltpu.SemaphoreType.DMA
        band = pl.pallas_call(
            functools.partial(square_kernel, n_row),
            out_shape=jax.ShapeDtypeStruct((3, panel, piece), f32),
            in_specs=[pl.BlockSpec(memory_space=pl.ANY), pl.BlockSpec(memory_space=pltpu.VMEM),
                      pl.BlockSpec(memory_space=pl.ANY)],
            out_specs=pl.BlockSpec(memory_space=pl.ANY),
            scratch_shapes=[
                pltpu.VMEM((3, chunks, rows, 2 * LANES), bf16),
                pltpu.VMEM((panel, rows), bf16),
                pltpu.VMEM((rows, 2 * LANES), bf16),
                pltpu.VMEM((2, panel, LANES), f32),
                pltpu.VMEM((4, panel, LANES), f32),
                pltpu.VMEM((7, panel, LANES), f32),
                pltpu.VMEM((3 * pairs, panel, LANES), bf16),
                pltpu.VMEM((3 * parts, panel, LANES), bf16),
                pltpu.VMEM((4, panel, LANES), bf16),
                pltpu.VMEM((2, rows, 2 * LANES), jnp.int32),
                pltpu.VMEM((n_row, 1, panel), f32),
                pltpu.VMEM((8, panel), f32),
                pltpu.VMEM((3, 8, panel), f32),
                pltpu.VMEM((panel, LANES), f32),
                dma((chunks, 2)), dma((2, 2)), dma((n_row,)), dma((n_row,)), dma((3,)), dma((3,)),
                dma((chunks, 2)), dma((chunks, 2)), dma((chunks, 2)), dma((chunks, 2)),
                dma((2,)), dma((4,)), dma((4,)), dma((3 * pairs,)), dma((3 * parts,)), dma((7,)),
                pltpu.SemaphoreType.REGULAR((3 * pairs,)),
            ],
            compiler_params=pltpu.CompilerParams(
                collective_id=0, has_side_effects=True, vmem_limit_bytes=67_043_328),
        )(data, column_scale[None, :], keep_mask)
        return band.transpose(1, 0, 2)

    return on_device


def solution(mesh):
    in_specs = (P("row", "col"), P("col"), P("row", "col"))
    out_specs = P("col", None, "row")

    def mapped(body):
        return jax.shard_map(
            body, mesh=mesh, in_specs=in_specs, out_specs=out_specs, check_vma=False
        )

    if mesh.shape["col"] == 4 and mesh.shape["row"] == 8:
        return mapped(square_program(mesh.shape["row"]))
    return mapped(on_device)
```

profile of v0, /device:TPU:11, one launch (start us, length us, event | category | flops | bytes accessed | tf_op | source)
XLA Modules:
  0.0 284.8 jit_solution(858074996515219053)
XLA Ops:
  0.0 278.9 %shard_map.37 = f32[3,2048,256]{2,1,0:T(8,128)} custom-call(bf16[2048,2048]{1,0:T(8,128)(2,1)} %data.1, f32[1,2048]{1,0:T(1,128)} %bitcast.3, s32[2048,2048]{1,0:T(8,128)} %mask.1), custom_call_target="tpu_custom_call" | custom-call | tf_op jit(solution)/shard_map/pallas_call | solution.py:504
  278.9 5.9 %copy.5 = f32[2048,3,256]{2,0,1:T(8,128)} copy(f32[2048,3,256]{2,0,1:T(8,128)} %bitcast.2) | data formatting | bytes 12582912
where the time goes:
time: 290 us; the launch traced here: 285 us
  Pallas kernels  279 us (96%)
  local copies, waits for them, and re-layouts  5.89 us (2%)
    pallas_call x1, Pallas kernels, on_device(): pl.pallas_call(functools.partial(square_kernel, n_row), out_shape=jax.Sha...  279 us
    unnamed x1, local copies, waits for them, and re-layouts  5.89 us

commit v1 on v0

--- a/solution.py
+++ b/solution.py
@@ -127,9 +127,9 @@
 
 def square_kernel(
     n_row, data, scale, mask, out,
-    buf, own_t, chunk, swap_out, swap_in, hold, near, far, line, masks, sums, plain, vec, back,
+    buf, own_t, chunk, swap_out, swap_in, hold, near, far, line, turned, mirror, stage, masks, sums, plain, vec, back,
     data_sem, mask_sem, sum_send, sum_recv, vec_send, vec_recv, y_send, y_recv, x_send, x_recv,
-    swap_send, swap_recv, line_send, near_recv, far_recv, out_sem, near_free,
+    swap_send, swap_recv, line_send, near_recv, far_recv, turn_send, turn_recv, out_sem, stage_sem, near_free,
 ):
     c, r = lax.axis_index("col"), lax.axis_index("row")
     z, k = r // 2, r % 2
@@ -142,7 +142,8 @@
     block = rows // 4
     half = rows // 2
     last = 3 * chunks + 2
-    near_slots, hold_slots, line_slots = 3 * pairs, 7, 4
+    near_slots, hold_slots, line_slots, swap_slots = 3 * pairs, 6, 4, 3
+    tall = panel // pairs
     forwards = c % 2 == 0
     y_peer, x_peer = (c + 2) % 4, c + 1 - 2 * (c % 2)
     partner = 2 * (z + 1 - 2 * (z % 2)) + k
@@ -157,26 +158,40 @@
         return pl.multiple_of(start, LANES)
 
     def stage_of(m):
-        offset = m % 3
-        return offset, m // 3 - jnp.where(offset == 1, 1, 0)
+        offset, turn = m % 3, m // 3
+        ahead = jnp.where(m == 1, 1, (turn + 2) % chunks)
+        own = jnp.logical_or(m == 1, offset == 0)
+        return jnp.where(own, 0, offset), jnp.where(own, ahead, turn - jnp.where(offset == 1, 1, 0))
 
     def valid(m):
-        return (m >= 0) & (m < last) & (m != 1) & (m != last - 2)
+        return (m >= 0) & (m < last) & (m != last - 5) & (m != last - 2)
+
+    def near_slot(m):
+        return jnp.where(m == 1, near_slots, m % near_slots)
+
+    def blocks_of(offset, q):
+        return jnp.where(offset == 0, target_of(q) + 1, pairs)
+
+    def rows_of(g):
+        return pl.ds(pl.multiple_of(g * tall, tall), tall)
 
     def role_of(q):
         goal = target_of(q)
         same = z // 2 == goal // 2
         return jnp.where(z == goal, 3, jnp.where(same, 1, jnp.where(inner, 2, 1)))
 
-    def data_copy(q, side):
-        return pltpu.make_async_copy(
-            data.at[:, pl.ds(column_of(q, k if side == 0 else 1 - k), LANES)],
-            buf.at[0, q, :, pl.ds(side * LANES, LANES)], data_sem.at[q, side])
-
-    def mask_copy(q, side):
-        return pltpu.make_async_copy(
-            mask.at[:, pl.ds(column_of(q, k if side == 0 else 1 - k), LANES)],
-            masks.at[q % 2, :, pl.ds(side * LANES, LANES)], mask_sem.at[q % 2, side])
+    def strip_of(u):
+        q, side = u // 2, u % 2
+        to = pl.ds(pl.multiple_of(side * LANES, LANES), LANES)
+        return q, to, pl.ds(column_of(q, k + side - 2 * k * side), LANES)
+
+    def data_copy(u):
+        q, to, columns = strip_of(u)
+        return pltpu.make_async_copy(data.at[:, columns], buf.at[0, q, :, to], data_sem.at[u])
+
+    def mask_copy(u):
+        _, _, columns = strip_of(u)
+        return pltpu.make_async_copy(mask.at[:, columns], masks.at[u % 2], mask_sem.at[u % 2])
 
     def half_of(offset, q, part):
         return buf.at[offset, q, pl.ds(part * half, half), :]
@@ -199,14 +214,12 @@
             def _():
                 x_copy(q, part, 0).start()
 
-    @pl.loop(0, chunks)
-    def _(q):
-        for side in range(2):
-            data_copy(q, side).start()
-
-    for q in range(2):
-        for side in range(2):
-            mask_copy(q, side).start()
+    mask_copy(0).start()
+    mask_copy(1).start()
+
+    @pl.loop(0, 2 * chunks)
+    def _(u):
+        data_copy(u).start()
 
     barrier = pltpu.get_barrier_semaphore()
     for step in range(1, n_row):
@@ -215,36 +228,32 @@
         pl.semaphore_signal(barrier, inc=1, device_id=((c + step) % 4, r), device_id_type=MESH_ID)
     pl.semaphore_wait(barrier, n_row + 2)
 
-    @pl.loop(0, chunks)
-    def _(q):
-        for side in range(2):
-            data_copy(q, side).wait()
-            mask_copy(q, side).wait()
-        scales = jnp.concatenate(
-            [scale[:, pl.ds(column_of(q, k), LANES)], scale[:, pl.ds(column_of(q, 1 - k), LANES)]], axis=1)
-        step = 128
+    @pl.loop(0, 2 * chunks)
+    def _(u):
+        data_copy(u).wait()
+        mask_copy(u).wait()
+        q, to, columns = strip_of(u)
+        scales = scale[:, columns]
+        step = 256
 
         def read(b, total):
             at = pl.ds(pl.multiple_of(b * step, step), step)
-            values = buf[0, q, at, :].astype(jnp.float32)
-            kept = masks[q % 2, at, :].astype(jnp.float32) * values
-            buf[0, q, at, :] = kept.astype(jnp.bfloat16)
+            values = buf[0, q, at, to].astype(jnp.float32)
+            kept = masks[u % 2, at, :].astype(jnp.float32) * values
+            buf[0, q, at, to] = kept.astype(jnp.bfloat16)
             values = values * scales
-            return total + jnp.sum((values * values).reshape(step // 8, 8, wide), axis=0)
-
-        total = lax.fori_loop(0, rows // step, read, jnp.zeros((8, wide), jnp.float32))
-        total = jnp.sum(total, axis=0, keepdims=True)
-        sums[r, :, pl.ds(column_of(q, k), LANES)] = total[:, :LANES]
-        sums[r, :, pl.ds(column_of(q, 1 - k), LANES)] = total[:, LANES:]
-
-        @pl.when(q + 2 < chunks)
-        def _():
-            for side in range(2):
-                mask_copy(q + 2, side).start()
-
-        @pl.when(q == 0)
-        def _():
-            start_own(q)
+            return total + jnp.sum((values * values).reshape(step // 8, 8, LANES), axis=0)
+
+        total = lax.fori_loop(0, rows // step, read, jnp.zeros((8, LANES), jnp.float32))
+        sums[r, :, columns] = jnp.sum(total, axis=0, keepdims=True)
+
+        @pl.when(u + 2 < 2 * chunks)
+        def _():
+            mask_copy(u + 2).start()
+
+        @pl.when(u == 1)
+        def _():
+            start_own(0)
 
     def sum_copy(step):
         peer = (r + step) % n_row
@@ -311,45 +320,51 @@
 
             back[pl.ds(column, LANES), :] = jnp.broadcast_to(factors[1:2, :], (LANES, LANES)).T
 
-    for offset in (2, 1):
-        vec_copy(offset).wait_recv()
-
-    tall = panel // 4
-
-    def swap_copy(m):
-        return pltpu.make_async_remote_copy(
-            swap_out.at[m % 2], swap_in.at[m % 4], swap_send.at[m % 2], swap_recv.at[m % 4],
+    def swap_copy(m, g):
+        return pltpu.make_async_remote_copy(
+            swap_out.at[m % 2, rows_of(g)], swap_in.at[m % swap_slots, rows_of(g)],
+            swap_send.at[m % 2, g], swap_recv.at[m % swap_slots, g],
             device_id=(c, 2 * z + 1 - k), device_id_type=MESH_ID)
 
-    def near_copy(m):
-        return pltpu.make_async_remote_copy(
-            line.at[m % line_slots], near.at[m % near_slots],
-            line_send.at[m % line_slots], near_recv.at[m % near_slots],
+    def near_copy(m, g):
+        return pltpu.make_async_remote_copy(
+            line.at[m % line_slots, rows_of(g)], near.at[near_slot(m), rows_of(g)],
+            line_send.at[m % line_slots, g], near_recv.at[near_slot(m), g],
             device_id=(c, partner), device_id_type=MESH_ID)
 
-    def far_copy(m, offset, q):
+    def far_copy(m, offset, q, g):
         slot = offset * parts + q // pairs
         return pltpu.make_async_remote_copy(
-            line.at[m % line_slots], far.at[slot], line_send.at[m % line_slots], far_recv.at[slot],
+            line.at[m % line_slots, rows_of(g)], far.at[slot, rows_of(g)],
+            line_send.at[m % line_slots, g], far_recv.at[slot, g],
             device_id=(c, 2 * target_of(q) + k), device_id_type=MESH_ID)
 
-    def out_copy(m, offset, q):
+    def out_copy(m, offset, q, g):
         lanes = pl.ds(pl.multiple_of((q // pairs) * LANES, LANES), LANES)
         return pltpu.make_async_copy(
-            hold.at[m % hold_slots], out.at[offset, :, lanes], out_sem.at[m % hold_slots])
-
-    def give_back(m):
-        @pl.when(valid(m + near_slots))
-        def _():
-            pl.semaphore_signal(
-                near_free.at[m % near_slots], inc=1, device_id=(c, partner), device_id_type=MESH_ID)
-
-    def in_blocks(body):
-        step = 256
-
-        @pl.loop(0, panel // step)
-        def _(b):
-            body(pl.ds(pl.multiple_of(b * step, step), step))
+            hold.at[m % hold_slots, rows_of(g)], out.at[offset, rows_of(g), lanes],
+            out_sem.at[m % hold_slots, g])
+
+    def turn_copy(part, g, core):
+        return pltpu.make_async_remote_copy(
+            turned.at[part, g, core], mirror.at[z - 1, k, part],
+            turn_send.at[part, g, core], turn_recv.at[z - 1, k, part],
+            device_id=(c, 2 * g + core), device_id_type=MESH_ID)
+
+    def turn_arrival(goal, core, part):
+        return pltpu.make_async_remote_copy(
+            turned.at[0, 0, 0], mirror.at[goal - 1, core, part],
+            turn_send.at[0, 0, 0], turn_recv.at[goal - 1, core, part],
+            device_id=(c, 2 * goal + core), device_id_type=MESH_ID)
+
+    def stage_copy(e, start):
+        return pltpu.make_async_copy(
+            stage.at[e % 2], out.at[0, pl.ds(start, LANES), :], stage_sem.at[e % 2])
+
+    def mirrored(e):
+        goal, core, part = e // (2 * parts) + 1, (e // parts) % 2, e % parts
+        start = pl.multiple_of((2 * goal + core) * piece + part * LANES, LANES)
+        return goal, core, part, start
 
     @pl.loop(0, last + hold_slots)
     def _(n):
@@ -358,15 +373,22 @@
 
             @pl.when(valid(m))
             def _():
-                action(offset, q)
-
-        def close_swap(offset, q):
-            swap_copy(n - 2).wait_send()
-
-        def close_out(offset, q):
+                @pl.loop(0, blocks_of(offset, q))
+                def _(g):
+                    action(offset, q, g)
+
+        def close_swap(offset, q, g):
+            swap_copy(n - 2, g).wait_send()
+
+        def close_out(offset, q, g):
             @pl.when(role_of(q) == 3)
             def _():
-                out_copy(n - hold_slots, offset, q).wait()
+                out_copy(n - hold_slots, offset, q, g).wait()
+
+        def close_line(offset, q, g):
+            @pl.when(role_of(q) != 3)
+            def _():
+                near_copy(n - 1 - line_slots, g).wait_send()
 
         settle(n - 2, close_swap)
         settle(n - hold_slots, close_out)
@@ -387,7 +409,18 @@
         def _():
             arrive(1)
 
-        def multiply(offset, q):
+        @pl.when(n == 2)
+        def _():
+            vec_copy(2).wait_recv()
+
+        @pl.when(n == 4)
+        def _():
+            vec_copy(1).wait_recv()
+
+        @pl.when(valid(n))
+        def _():
+            offset, q = stage_of(n)
+
             @pl.when(offset == 1)
             def _():
                 for part in range(2):
@@ -400,87 +433,112 @@
                 at = pl.ds(pl.multiple_of(b * block, block), block)
                 chunk[at, :] = (buf[offset, q, at, :].astype(jnp.float32) * factors).astype(jnp.bfloat16)
 
-            @pl.loop(0, panel // tall)
-            def _(b):
-                at = pl.ds(pl.multiple_of(b * tall, tall), tall)
-                product = jnp.dot(own_t[at, :], chunk[...], preferred_element_type=jnp.float32)
-                hold[n % hold_slots, at, :] = product[:, :LANES]
-                swap_out[n % 2, at, :] = product[:, LANES:]
-
-            swap_copy(n).start()
-
-        settle(n, multiply)
-
-        def join(offset, q):
+        settle(n - 1 - line_slots, close_line)
+
+        def join(offset, q, g):
             m = n - 1
-            swap_copy(m).wait_recv()
+            at = rows_of(g)
             role = role_of(q)
+            swap_copy(m, g).wait_recv()
 
             @pl.when(role == 1)
             def _():
-                def body(at):
-                    line[m % line_slots, at, :] = sent(hold[m % hold_slots, at, :] + swap_in[m % 4, at, :])
-
-                in_blocks(body)
-
-                @pl.when(valid(m - near_slots))
+                line[m % line_slots, at, :] = sent(hold[m % hold_slots, at, :] + swap_in[m % swap_slots, at, :])
+
+                @pl.when((g == 0) & (m >= near_slots) & valid(m - near_slots) & (m != near_slots + 1))
                 def _():
                     pl.semaphore_wait(near_free.at[m % near_slots], 1)
 
-                near_copy(m).start()
+                near_copy(m, g).start()
 
             @pl.when(role != 1)
             def _():
-                def body(at):
-                    hold[m % hold_slots, at, :] = hold[m % hold_slots, at, :] + swap_in[m % 4, at, :]
-
-                in_blocks(body)
-
-        def close_line(offset, q):
-            @pl.when(role_of(q) != 3)
-            def _():
-                near_copy(n - 1 - line_slots).wait_send()
-
-        settle(n - 1 - line_slots, close_line)
+                hold[m % hold_slots, at, :] = hold[m % hold_slots, at, :] + swap_in[m % swap_slots, at, :]
+
         settle(n - 1, join)
 
-        def relay(offset, q):
+        def multiply(offset, q, g):
+            at = rows_of(g)
+            product = jnp.dot(own_t[at, :], chunk[...], preferred_element_type=jnp.float32)
+            hold[n % hold_slots, at, :] = product[:, :LANES]
+            swap_out[n % 2, at, :] = product[:, LANES:]
+            swap_copy(n, g).start()
+
+        settle(n, multiply)
+
+        def give_back(m, offset, q, g):
+            @pl.when((g == blocks_of(offset, q) - 1) & valid(m + near_slots) & (m != 1))
+            def _():
+                pl.semaphore_signal(
+                    near_free.at[m % near_slots], inc=1, device_id=(c, partner), device_id_type=MESH_ID)
+
+        def relay(offset, q, g):
             m = n - 3
+            at = rows_of(g)
 
             @pl.when(role_of(q) == 2)
             def _():
-                near_copy(m).wait_recv()
-
-                def body(at):
-                    line[m % line_slots, at, :] = sent(
-                        hold[m % hold_slots, at, :] + received(near[m % near_slots, at, :]))
-
-                in_blocks(body)
-                give_back(m)
-                far_copy(m, offset, q).start()
+                near_copy(m, g).wait_recv()
+                line[m % line_slots, at, :] = sent(
+                    hold[m % hold_slots, at, :] + received(near[near_slot(m), at, :]))
+                give_back(m, offset, q, g)
+                far_copy(m, offset, q, g).start()
 
         settle(n - 3, relay)
 
-        def finish(offset, q):
+        def finish(offset, q, g):
             m = n - 5
+            at = rows_of(g)
 
             @pl.when(role_of(q) == 3)
             def _():
-                near_copy(m).wait_recv()
-                far_copy(m, offset, q).wait_recv()
-                slot = offset * parts + q // pairs
+                near_copy(m, g).wait_recv()
+                far_copy(m, offset, q, g).wait_recv()
+                part = q // pairs
                 factors = vec[offset, 1:2, pl.ds(pl.multiple_of(q * wide, wide), LANES)]
-
-                def body(at):
-                    total = hold[m % hold_slots, at, :] + received(near[m % near_slots, at, :])
-                    total = total + received(far[slot, at, :])
-                    hold[m % hold_slots, at, :] = total * back[at, :] * factors
-
-                in_blocks(body)
-                give_back(m)
-                out_copy(m, offset, q).start()
+                total = hold[m % hold_slots, at, :] + received(near[near_slot(m), at, :])
+                total = total + received(far[offset * parts + part, at, :])
+                hold[m % hold_slots, at, :] = total * back[at, :] * factors
+                give_back(m, offset, q, g)
+                out_copy(m, offset, q, g).start()
+
+                @pl.when((offset == 0) & (g < z))
+                def _():
+                    across = sent(total).T
+                    for core in range(2):
+                        turned[part, g, core] = across[:, core * piece:(core + 1) * piece]
+                        turn_copy(part, g, core).start()
 
         settle(n - 5, finish)
+
+        @pl.when(n == last + 1)
+        def _():
+            factors = plain[1:2, pl.ds(pl.multiple_of(r * piece, piece), piece)]
+
+            @pl.loop(2 * parts * z, 2 * parts * (pairs - 1))
+            def _(e):
+                goal, core, part, start = mirrored(e)
+                turn_arrival(goal, core, part).wait_recv()
+
+                @pl.when(e >= 2 * parts * z + 2)
+                def _():
+                    stage_copy(e - 2, mirrored(e - 2)[3]).wait()
+
+                sizes = back[pl.ds(start, LANES), :]
+                sizes = jnp.concatenate([sizes] * (piece // LANES), axis=1)
+                stage[e % 2] = received(mirror[goal - 1, core, part]) * sizes * factors
+                stage_copy(e, start).start()
+
+    @pl.when(z < pairs - 1)
+    def _():
+        for e in range(2 * parts * (pairs - 1) - 2, 2 * parts * (pairs - 1)):
+            stage_copy(e, mirrored(e)[3]).wait()
+
+    @pl.loop(0, z)
+    def _(g):
+        for part in range(parts):
+            for core in range(2):
+                turn_copy(part, g, core).wait_send()
 
     @pl.loop(0, chunks)
     def _(q):
@@ -512,20 +570,24 @@
                 pltpu.VMEM((panel, rows), bf16),
                 pltpu.VMEM((rows, 2 * LANES), bf16),
                 pltpu.VMEM((2, panel, LANES), f32),
-                pltpu.VMEM((4, panel, LANES), f32),
-                pltpu.VMEM((7, panel, LANES), f32),
-                pltpu.VMEM((3 * pairs, panel, LANES), bf16),
+                pltpu.VMEM((3, panel, LANES), f32),
+                pltpu.VMEM((6, panel, LANES), f32),
+                pltpu.VMEM((3 * pairs + 1, panel, LANES), bf16),
                 pltpu.VMEM((3 * parts, panel, LANES), bf16),
                 pltpu.VMEM((4, panel, LANES), bf16),
-                pltpu.VMEM((2, rows, 2 * LANES), jnp.int32),
+                pltpu.VMEM((parts, pairs - 1, 2, LANES, piece), bf16),
+                pltpu.VMEM((pairs - 1, 2, parts, LANES, piece), bf16),
+                pltpu.VMEM((2, LANES, piece), f32),
+                pltpu.VMEM((2, rows, LANES), jnp.int32),
                 pltpu.VMEM((n_row, 1, panel), f32),
                 pltpu.VMEM((8, panel), f32),
                 pltpu.VMEM((3, 8, panel), f32),
                 pltpu.VMEM((panel, LANES), f32),
-                dma((chunks, 2)), dma((2, 2)), dma((n_row,)), dma((n_row,)), dma((3,)), dma((3,)),
+                dma((2 * chunks,)), dma((2,)), dma((n_row,)), dma((n_row,)), dma((3,)), dma((3,)),
                 dma((chunks, 2)), dma((chunks, 2)), dma((chunks, 2)), dma((chunks, 2)),
-                dma((2,)), dma((4,)), dma((4,)), dma((3 * pairs,)), dma((3 * parts,)), dma((7,)),
-                pltpu.SemaphoreType.REGULAR((3 * pairs,)),
+                dma((2, pairs)), dma((3, pairs)), dma((4, pairs)), dma((3 * pairs + 1, pairs)),
+                dma((3 * parts, pairs)), dma((parts, pairs - 1, 2)), dma((pairs - 1, 2, parts)),
+                dma((6, pairs)), dma((2,)), pltpu.SemaphoreType.REGULAR((3 * pairs,)),
             ],
             compiler_params=pltpu.CompilerParams(
                 collective_id=0, has_side_effects=True, vmem_limit_bytes=67_043_328),

time: 290 us -> 254 us (0.88)
  Pallas kernels: 279 us -> 243 us
    pallas_call x1, Pallas kernels: 279 us -> 243 us  [on_device(): pl.pallas_call(functools.partial(square_kernel, n_row), out_shape=jax.Sha...]
where the time goes in v1:
time: 254 us; the launch traced here: 249 us
  Pallas kernels  243 us (96%)
  local copies, waits for them, and re-layouts  5.89 us (2%)
    pallas_call x1, Pallas kernels, on_device(): pl.pallas_call(functools.partial(square_kernel, n_row), out_shape=jax.Sha...  243 us
    unnamed x1, local copies, waits for them, and re-layouts  5.89 us

profile of v1, /device:TPU:11, one launch (start us, length us, event | category | flops | bytes accessed | tf_op | source)
XLA Modules:
  0.0 248.8 jit_solution(17402765668872020941)
XLA Ops:
  0.0 242.9 %shard_map.37 = f32[3,2048,256]{2,1,0:T(8,128)} custom-call(bf16[2048,2048]{1,0:T(8,128)(2,1)} %data.1, f32[1,2048]{1,0:T(1,128)} %bitcast.3, s32[2048,2048]{1,0:T(8,128)} %mask.1), custom_call_target="tpu_custom_call" | custom-call | tf_op jit(solution)/shard_map/pallas_call | solution.py:562
  242.9 5.9 %copy.5 = f32[2048,3,256]{2,0,1:T(8,128)} copy(f32[2048,3,256]{2,0,1:T(8,128)} %bitcast.2) | data formatting | bytes 12582912

commit v2 on v1

--- a/solution.py
+++ b/solution.py
@@ -140,9 +140,10 @@
     parts = piece // LANES
     chunks = pairs * parts
     block = rows // 4
-    half = rows // 2
+    pieces = 4
+    cut = rows // pieces
     last = 3 * chunks + 2
-    near_slots, hold_slots, line_slots, swap_slots = 3 * pairs, 6, 4, 3
+    near_slots, hold_slots, line_slots, swap_slots = 3 * pairs, 7, 5, 3
     tall = panel // pairs
     forwards = c % 2 == 0
     y_peer, x_peer = (c + 2) % 4, c + 1 - 2 * (c % 2)
@@ -151,7 +152,7 @@
 
     def target_of(q):
         at = q % pairs
-        return jnp.where(at == 0, 0, jnp.where(at == 1, 3, at - 1))
+        return jnp.where(at == 0, 0, jnp.where(at == 1, 3, jnp.where(at == 2, 2, 1)))
 
     def column_of(q, core):
         start = (2 * target_of(q) + core) * piece + (q // pairs) * LANES
@@ -159,7 +160,7 @@
 
     def stage_of(m):
         offset, turn = m % 3, m // 3
-        ahead = jnp.where(m == 1, 1, (turn + 2) % chunks)
+        ahead = jnp.where(m == 1, 0, (turn + 1) % chunks)
         own = jnp.logical_or(m == 1, offset == 0)
         return jnp.where(own, 0, offset), jnp.where(own, ahead, turn - jnp.where(offset == 1, 1, 0))
 
@@ -180,6 +181,8 @@
         same = z // 2 == goal // 2
         return jnp.where(z == goal, 3, jnp.where(same, 1, jnp.where(inner, 2, 1)))
 
+    ahead = 3
+
     def strip_of(u):
         q, side = u // 2, u % 2
         to = pl.ds(pl.multiple_of(side * LANES, LANES), LANES)
@@ -191,33 +194,34 @@
 
     def mask_copy(u):
         _, _, columns = strip_of(u)
-        return pltpu.make_async_copy(mask.at[:, columns], masks.at[u % 2], mask_sem.at[u % 2])
-
-    def half_of(offset, q, part):
-        return buf.at[offset, q, pl.ds(part * half, half), :]
+        return pltpu.make_async_copy(mask.at[:, columns], masks.at[u % ahead], mask_sem.at[u % ahead])
+
+    def cut_of(offset, q, part):
+        return buf.at[offset, q, pl.ds(part * cut, cut), :]
 
     def y_copy(q, part):
         return pltpu.make_async_remote_copy(
-            half_of(0, q, part), half_of(2, q, part), y_send.at[q, part], y_recv.at[q, part],
+            cut_of(0, q, part), cut_of(2, q, part), y_send.at[q, part], y_recv.at[q, part],
             device_id=(y_peer, r), device_id_type=MESH_ID)
 
     def x_copy(q, part, source):
         return pltpu.make_async_remote_copy(
-            half_of(source, q, part), half_of(1, q, part), x_send.at[q, part], x_recv.at[q, part],
+            cut_of(source, q, part), cut_of(1, q, part), x_send.at[q, part], x_recv.at[q, part],
             device_id=(x_peer, r), device_id_type=MESH_ID)
 
     def start_own(q):
-        for part in range(2):
+        for part in range(pieces):
             y_copy(q, part).start()
 
             @pl.when(jnp.logical_not(forwards))
             def _():
                 x_copy(q, part, 0).start()
 
-    mask_copy(0).start()
-    mask_copy(1).start()
-
-    @pl.loop(0, 2 * chunks)
+    for u in range(ahead):
+        data_copy(u).start()
+        mask_copy(u).start()
+
+    @pl.loop(ahead, 2 * chunks)
     def _(u):
         data_copy(u).start()
 
@@ -233,23 +237,22 @@
         data_copy(u).wait()
         mask_copy(u).wait()
         q, to, columns = strip_of(u)
-        scales = scale[:, columns]
         step = 256
 
         def read(b, total):
             at = pl.ds(pl.multiple_of(b * step, step), step)
             values = buf[0, q, at, to].astype(jnp.float32)
-            kept = masks[u % 2, at, :].astype(jnp.float32) * values
+            kept = masks[u % ahead, at, :].astype(jnp.float32) * values
             buf[0, q, at, to] = kept.astype(jnp.bfloat16)
-            values = values * scales
             return total + jnp.sum((values * values).reshape(step // 8, 8, LANES), axis=0)
 
         total = lax.fori_loop(0, rows // step, read, jnp.zeros((8, LANES), jnp.float32))
-        sums[r, :, columns] = jnp.sum(total, axis=0, keepdims=True)
-
-        @pl.when(u + 2 < 2 * chunks)
-        def _():
-            mask_copy(u + 2).start()
+        scales = scale[:, columns]
+        sums[r, :, columns] = jnp.sum(total, axis=0, keepdims=True) * scales * scales
+
+        @pl.when(u + ahead < 2 * chunks)
+        def _():
+            mask_copy(u + ahead).start()
 
         @pl.when(u == 1)
         def _():
@@ -305,6 +308,16 @@
     def _(q):
         start_own(q)
 
+    def arrive(q, part):
+        y_copy(q, part).wait_recv()
+
+        @pl.when(forwards)
+        def _():
+            x_copy(q, part, 2).start()
+
+    arrive(0, 0)
+    arrive(0, 1)
+
     @pl.loop(0, chunks)
     def _(q):
         for side in range(2):
@@ -393,21 +406,15 @@
         settle(n - 2, close_swap)
         settle(n - hold_slots, close_out)
 
-        def arrive(part):
-            q = n // 3
-            y_copy(q, part).wait_recv()
-
-            @pl.when(forwards)
-            def _():
-                x_copy(q, part, 2).start()
-
-        @pl.when((n % 3 == 1) & (n // 3 < chunks))
-        def _():
-            arrive(0)
-
-        @pl.when((n % 3 == 2) & (n // 3 < chunks))
-        def _():
-            arrive(1)
+        turn = n // 3
+
+        @pl.when((n % 3 == 1) & (turn > 0) & (turn < chunks))
+        def _():
+            arrive(turn, 1)
+
+        @pl.when((n % 3 == 2) & (turn < chunks))
+        def _():
+            arrive(turn, 3)
 
         @pl.when(n == 2)
         def _():
@@ -423,7 +430,7 @@
 
             @pl.when(offset == 1)
             def _():
-                for part in range(2):
+                for part in range(pieces):
                     x_copy(q, part, 0).wait_recv()
 
             factors = vec[offset, 0:1, pl.ds(pl.multiple_of(q * wide, wide), wide)]
@@ -456,6 +463,14 @@
                 hold[m % hold_slots, at, :] = hold[m % hold_slots, at, :] + swap_in[m % swap_slots, at, :]
 
         settle(n - 1, join)
+
+        @pl.when((n % 3 == 0) & (turn > 0) & (turn < chunks))
+        def _():
+            arrive(turn, 0)
+
+        @pl.when((n % 3 == 1) & (turn < chunks))
+        def _():
+            arrive(turn, 2)
 
         def multiply(offset, q, g):
             at = rows_of(g)
@@ -487,7 +502,7 @@
         settle(n - 3, relay)
 
         def finish(offset, q, g):
-            m = n - 5
+            m = n - 6
             at = rows_of(g)
 
             @pl.when(role_of(q) == 3)
@@ -509,7 +524,7 @@
                         turned[part, g, core] = across[:, core * piece:(core + 1) * piece]
                         turn_copy(part, g, core).start()
 
-        settle(n - 5, finish)
+        settle(n - 6, finish)
 
         @pl.when(n == last + 1)
         def _():
@@ -542,7 +557,7 @@
 
     @pl.loop(0, chunks)
     def _(q):
-        for part in range(2):
+        for part in range(pieces):
             y_copy(q, part).wait_send()
             x_copy(q, part, 0).wait_send()
 
@@ -571,23 +586,23 @@
                 pltpu.VMEM((rows, 2 * LANES), bf16),
                 pltpu.VMEM((2, panel, LANES), f32),
                 pltpu.VMEM((3, panel, LANES), f32),
-                pltpu.VMEM((6, panel, LANES), f32),
+                pltpu.VMEM((7, panel, LANES), f32),
                 pltpu.VMEM((3 * pairs + 1, panel, LANES), bf16),
                 pltpu.VMEM((3 * parts, panel, LANES), bf16),
-                pltpu.VMEM((4, panel, LANES), bf16),
+                pltpu.VMEM((5, panel, LANES), bf16),
                 pltpu.VMEM((parts, pairs - 1, 2, LANES, piece), bf16),
                 pltpu.VMEM((pairs - 1, 2, parts, LANES, piece), bf16),
                 pltpu.VMEM((2, LANES, piece), f32),
-                pltpu.VMEM((2, rows, LANES), jnp.int32),
+                pltpu.VMEM((3, rows, LANES), jnp.int32),
                 pltpu.VMEM((n_row, 1, panel), f32),
                 pltpu.VMEM((8, panel), f32),
                 pltpu.VMEM((3, 8, panel), f32),
                 pltpu.VMEM((panel, LANES), f32),
-                dma((2 * chunks,)), dma((2,)), dma((n_row,)), dma((n_row,)), dma((3,)), dma((3,)),
-                dma((chunks, 2)), dma((chunks, 2)), dma((chunks, 2)), dma((chunks, 2)),
-                dma((2, pairs)), dma((3, pairs)), dma((4, pairs)), dma((3 * pairs + 1, pairs)),
+                dma((2 * chunks,)), dma((4,)), dma((n_row,)), dma((n_row,)), dma((3,)), dma((3,)),
+                dma((chunks, 4)), dma((chunks, 4)), dma((chunks, 4)), dma((chunks, 4)),
+                dma((2, pairs)), dma((3, pairs)), dma((5, pairs)), dma((3 * pairs + 1, pairs)),
                 dma((3 * parts, pairs)), dma((parts, pairs - 1, 2)), dma((pairs - 1, 2, parts)),
-                dma((6, pairs)), dma((2,)), pltpu.SemaphoreType.REGULAR((3 * pairs,)),
+                dma((7, pairs)), dma((2,)), pltpu.SemaphoreType.REGULAR((3 * pairs,)),
             ],
             compiler_params=pltpu.CompilerParams(
                 collective_id=0, has_side_effects=True, vmem_limit_bytes=67_043_328),

time: 254 us -> 240 us (0.945); the launches traced: 249 us -> 238 us
  Pallas kernels: 243 us -> 232 us
    pallas_call x1, Pallas kernels: 243 us -> 232 us  [on_device(): pl.pallas_call(functools.partial(square_kernel, n_row), out_shape=jax.Sha...]
where the time goes in v2:
time: 240 us; the launch traced here: 238 us
  Pallas kernels  232 us (97%)
  local copies, waits for them, and re-layouts  5.89 us (2%)
    pallas_call x1, Pallas kernels, on_device(): pl.pallas_call(functools.partial(square_kernel, n_row), out_shape=jax.Sha...  232 us
    unnamed x1, local copies, waits for them, and re-layouts  5.89 us

profile of v2, /device:TPU:11, one launch (start us, length us, event | category | flops | bytes accessed | tf_op | source)
XLA Modules:
  0.0 237.9 jit_solution(16393163422397553023)
XLA Ops:
  0.0 232.0 %shard_map.37 = f32[3,2048,256]{2,1,0:T(8,128)} custom-call(bf16[2048,2048]{1,0:T(8,128)(2,1)} %data.1, f32[1,2048]{1,0:T(1,128)} %bitcast.3, s32[2048,2048]{1,0:T(8,128)} %mask.1), custom_call_target="tpu_custom_call" | custom-call | tf_op jit(solution)/shard_map/pallas_call | solution.py:577
  232.0 5.9 %copy.5 = f32[2048,3,256]{2,0,1:T(8,128)} copy(f32[2048,3,256]{2,0,1:T(8,128)} %bitcast.2) | data formatting | bytes 12582912

commit v3 on v2

--- a/solution.py
+++ b/solution.py
@@ -143,7 +143,7 @@
     pieces = 4
     cut = rows // pieces
     last = 3 * chunks + 2
-    near_slots, hold_slots, line_slots, swap_slots = 3 * pairs, 7, 5, 3
+    near_slots, hold_slots, line_slots, swap_slots = 3 * pairs, 6, 5, 3
     tall = panel // pairs
     forwards = c % 2 == 0
     y_peer, x_peer = (c + 2) % 4, c + 1 - 2 * (c % 2)
@@ -152,7 +152,7 @@
 
     def target_of(q):
         at = q % pairs
-        return jnp.where(at == 0, 0, jnp.where(at == 1, 3, jnp.where(at == 2, 2, 1)))
+        return jnp.where(at == 0, 0, jnp.where(at == 1, 2, jnp.where(at == 2, 3, 1)))
 
     def column_of(q, core):
         start = (2 * target_of(q) + core) * piece + (q // pairs) * LANES
@@ -488,7 +488,7 @@
                     near_free.at[m % near_slots], inc=1, device_id=(c, partner), device_id_type=MESH_ID)
 
         def relay(offset, q, g):
-            m = n - 3
+            m = n - 2
             at = rows_of(g)
 
             @pl.when(role_of(q) == 2)
@@ -499,10 +499,10 @@
                 give_back(m, offset, q, g)
                 far_copy(m, offset, q, g).start()
 
-        settle(n - 3, relay)
+        settle(n - 2, relay)
 
         def finish(offset, q, g):
-            m = n - 6
+            m = n - 5
             at = rows_of(g)
 
             @pl.when(role_of(q) == 3)
@@ -524,7 +524,7 @@
                         turned[part, g, core] = across[:, core * piece:(core + 1) * piece]
                         turn_copy(part, g, core).start()
 
-        settle(n - 6, finish)
+        settle(n - 5, finish)
 
         @pl.when(n == last + 1)
         def _():
@@ -586,7 +586,7 @@
                 pltpu.VMEM((rows, 2 * LANES), bf16),
                 pltpu.VMEM((2, panel, LANES), f32),
                 pltpu.VMEM((3, panel, LANES), f32),
-                pltpu.VMEM((7, panel, LANES), f32),
+                pltpu.VMEM((6, panel, LANES), f32),
                 pltpu.VMEM((3 * pairs + 1, panel, LANES), bf16),
                 pltpu.VMEM((3 * parts, panel, LANES), bf16),
                 pltpu.VMEM((5, panel, LANES), bf16),
@@ -602,7 +602,7 @@
                 dma((chunks, 4)), dma((chunks, 4)), dma((chunks, 4)), dma((chunks, 4)),
                 dma((2, pairs)), dma((3, pairs)), dma((5, pairs)), dma((3 * pairs + 1, pairs)),
                 dma((3 * parts, pairs)), dma((parts, pairs - 1, 2)), dma((pairs - 1, 2, parts)),
-                dma((7, pairs)), dma((2,)), pltpu.SemaphoreType.REGULAR((3 * pairs,)),
+                dma((6, pairs)), dma((2,)), pltpu.SemaphoreType.REGULAR((3 * pairs,)),
             ],
             compiler_params=pltpu.CompilerParams(
                 collective_id=0, has_side_effects=True, vmem_limit_bytes=67_043_328),

time: 240 us -> 239 us (level)
  no operation moved by 1% of the time
where the time goes in v3:
time: 239 us; the launch traced here: 237 us
  Pallas kernels  231 us (97%)
  local copies, waits for them, and re-layouts  5.89 us (2%)
    pallas_call x1, Pallas kernels, on_device(): pl.pallas_call(functools.partial(square_kernel, n_row), out_shape=jax.Sha...  231 us
    unnamed x1, local copies, waits for them, and re-layouts  5.89 us

profile of v3, /device:TPU:11, one launch (start us, length us, event | category | flops | bytes accessed | tf_op | source)
XLA Modules:
  0.0 236.5 jit_solution(11955524405435779131)
XLA Ops:
  0.0 230.6 %shard_map.37 = f32[3,2048,256]{2,1,0:T(8,128)} custom-call(bf16[2048,2048]{1,0:T(8,128)(2,1)} %data.1, f32[1,2048]{1,0:T(1,128)} %bitcast.3, s32[2048,2048]{1,0:T(8,128)} %mask.1), custom_call_target="tpu_custom_call" | custom-call | tf_op jit(solution)/shard_map/pallas_call | solution.py:577
  230.6 5.9 %copy.5 = f32[2048,3,256]{2,0,1:T(8,128)} copy(f32[2048,3,256]{2,0,1:T(8,128)} %bitcast.2) | data formatting | bytes 12582912
